TPU v7x, 256 devices: a whole 4x4x8 slice. The times are simulated.
256 devices in a mesh: req: 32 (over y, z), ctx: 8 (over x, core).
Axes of the slice: x: 4, y: 4, z: 8, core: 2. Of those that a mesh axis runs over, the one named last changes fastest.
Arguments:
- history: bfloat16 [196608, 1024], P(('req', 'ctx')), may hold values from -6 to 6
- block_owner: int32 [12288, 1], P(('req', 'ctx')), may hold values from 0 to 31; in each aligned block of 48 rows (0 to 47, 48 to 95, ...) at most 3 rows name the same one
- candidates: bfloat16 [32768, 1024], P(('req', 'ctx')), may hold values from -6 to 6
- w_kv: bfloat16 [1024, 2048], replicated, may hold values from -0.1875 to 0.1875
- w_qu: bfloat16 [1024, 2048], replicated, may hold values from -0.1875 to 0.1875
- w_out: bfloat16 [1024, 1024], replicated, may hold values from -0.1875 to 0.1875
Outputs:
- scored: bfloat16 [32768, 1024], P(('req', 'ctx'))
Inputs may be any that keep to these rules, and one draw needn't show every extreme that they name: `block_owner`: each packed block belongs to one request; among the 48 blocks of one device at most 3 belong to the same request, and that most is reached on some device; every request owns at least one block.
All inputs are finite; a program needn't handle non-finite values.
Results may differ from a plain program's by a relative error of at most 0.0052.
Values may be sent and summed in bfloat16 or wider, within the bound.
A program may use at most 128 MiB of HBM per device.

v0:
```python
import jax
import jax.numpy as jnp
from jax import lax
from jax.sharding import Mesh
from jax.sharding import PartitionSpec as P

HEAD = 128
CTX = ("ctx_0", "ctx_1")
REQ_CTX = ("req", "ctx_0", "ctx_1")


key_span = 512


def grouped_exchange(value, axis, split_dim, concat_dim, work, item_dim, out_dim):

    def moved(group):
        return lax.all_to_all(group, axis, split_axis=split_dim, concat_axis=concat_dim, tiled=True)

    items = jax.tree.leaves(value)[0].shape[item_dim]
    ends = [items * k // 2 for k in range(2 + 1)] if items % 2 == 0 else [0, items]
    groups = [
        jax.tree.map(lambda a: lax.slice_in_dim(a, low, high, axis=item_dim), value)
        for low, high in zip(ends, ends[1:])
    ]
    arrived = [moved(group) for group in groups]
    made = [work(group) for group in arrived]
    return jax.tree.map(lambda *parts: jnp.concatenate(parts, axis=out_dim), *made)


def edges_of(length, count):
    unit = 8 if length >= 8 * count else 1
    return [length // unit * k // count * unit for k in range(1, count)]


def all_blocks(value, axes, turns):
    parts = value
    for k in turns:
        parts = lax.all_gather(parts, axes[k])
    done = turns[::-1]
    back = [done.index(k) for k in range(len(axes))]
    parts = parts.transpose(*back, *range(len(axes), parts.ndim))
    return parts.reshape(-1, *value.shape)


def laid_out(parts, dim):
    parts = jnp.moveaxis(parts, 0, dim)
    shape = parts.shape
    return parts.reshape(*shape[:dim], shape[dim] * shape[dim + 1], *shape[dim + 2 :])


def gather_at_once(value, axes, dim):
    widest = max(range(max(1, value.ndim - 1)), key=lambda d: value.shape[d])
    count, finished = (len(axes), [])
    for first, piece in enumerate(
        jnp.split(value, edges_of(value.shape[widest], count), axis=widest)
    ):
        if piece.size:
            turns = [(first - k) % count for k in range(count)]
            finished.append(all_blocks(piece, axes, turns))
    return laid_out(jnp.concatenate(finished, axis=widest + 1), dim)


def cut_along(value, dim, length):
    before, after = (value.shape[:dim], value.shape[dim + 1 :])
    return jnp.moveaxis(value.reshape(*before, length, -1, *after), dim, 0)


def sum_at_owner(value, axis, dim):
    length = lax.axis_size(axis)
    parts = lax.all_to_all(cut_along(value, dim, length), axis, 0, 0, tiled=True)
    return jnp.sum(parts.astype(jnp.float32), axis=0)


def attend(queries, keys_values):
    count, width = queries.shape
    heads = width // HEAD
    rows = keys_values.shape[0]
    query = queries.reshape(count, heads, HEAD)
    pieces = keys_values.reshape(rows // key_span, key_span, 2, heads, HEAD)
    factor = HEAD ** (-0.5)

    def add_block(total, piece):
        scores = (
            jnp.einsum("qhd,khd->hqk", query, piece[:, 0], preferred_element_type=jnp.float32)
            * factor
        )
        weights = jax.nn.silu(scores).astype(jnp.bfloat16)
        return (
            total
            + jnp.einsum("hqk,khd->qhd", weights, piece[:, 1], preferred_element_type=jnp.float32),
            None,
        )

    total, _ = lax.scan(add_block, jnp.zeros((count, heads, HEAD), jnp.float32), pieces)
    return total.reshape(count, width)


def on_device(history, block_owner, candidates, w_kv, w_qu, w_out):
    owners_count = lax.axis_size("req")
    rows, width = history.shape
    blocks = block_owner.shape[0]
    events = rows // blocks
    capacity = 2 * blocks // owners_count
    owner = block_owner[:, 0]
    onehot = (owner[:, None] == jnp.arange(owners_count, dtype=jnp.int32)[None, :]).astype(
        jnp.int32
    )
    rank = jnp.sum((jnp.cumsum(onehot, axis=0) - onehot) * onehot, axis=1)
    slot = owner * capacity + rank
    placing = (
        slot[None, :] == jnp.arange(owners_count * capacity, dtype=jnp.int32)[:, None]
    ).astype(jnp.bfloat16)

    def project(raw):
        flat = raw.reshape(-1, raw.shape[-1])
        linear = jnp.dot(flat, w_kv, preferred_element_type=jnp.float32)
        half = linear.shape[-1] // 2
        made = jnp.concatenate([jax.nn.silu(linear[:, :half]), linear[:, half:]], axis=1).astype(
            jnp.bfloat16
        )
        return made.reshape(raw.shape[:-1] + (made.shape[-1],))

    packed = jnp.dot(
        placing, history.reshape(blocks, events * width), preferred_element_type=jnp.float32
    )
    packed = packed.astype(jnp.bfloat16).reshape(owners_count, capacity, events, width)
    arrived = grouped_exchange(packed, "req", 0, 0, project, 1, 1)
    context = arrived.reshape(-1, 2 * width)
    projected = jnp.dot(candidates, w_qu, preferred_element_type=jnp.float32)
    queries = jax.nn.silu(projected[:, :width]).astype(jnp.bfloat16)
    gate = jax.nn.silu(projected[:, width:])
    partial_value = attend(gather_at_once(queries, CTX, 0), context)
    attended = sum_at_owner(partial_value.astype(jnp.bfloat16), CTX, 0)
    mean = jnp.mean(attended, axis=-1, keepdims=True)
    centred = attended - mean
    variance = jnp.mean(centred * centred, axis=-1, keepdims=True)
    mixed = (centred * lax.rsqrt(variance + 1e-05) * gate).astype(jnp.bfloat16)
    result = candidates.astype(jnp.float32) + jnp.dot(
        mixed, w_out, preferred_element_type=jnp.float32
    )
    return result.astype(jnp.bfloat16)


def solution(mesh):
    torus = Mesh(mesh.devices.reshape(mesh.shape["req"], 4, 2), ("req", "ctx_0", "ctx_1"))
    in_specs = (P(REQ_CTX, None), P(REQ_CTX, None), P(REQ_CTX, None), P(), P(), P())
    out_specs = P(REQ_CTX, None)
    return jax.shard_map(
        on_device, mesh=torus, in_specs=in_specs, out_specs=out_specs, check_vma=False
    )
```

profile of v0, /device:TPU:1, one launch (start us, length us, event | category | flops | bytes accessed | tf_op | source)
XLA Modules:
  0.0 220.7 jit_solution(822562573387319791)
XLA Ops:
  6.5 0.0 copy-start
  6.5 0.9 fusion.12
  7.4 0.1 reduce_window_sum.11
  7.5 0.8 select_reduce_fusion
  8.3 0.7 multiply_add_fusion
  9.0 3.8 %reshape.41 = bf16[48,16384]{1,0:T(8,128)(2,1)} reshape(bf16[768,1024]{1,0:T(8,128)(2,1)} %param.8) | data formatting | bytes 3145728 | tf_op jit(solution)/shard_map/reshape | solution.py:125
  12.7 2.4 %convolution_convert_fusion = bf16[96,16384]{1,0:T(8,128)(2,1)S(1)} fusion(bf16[48,16384]{1,0:T(8,128)(2,1)} %reshape.41, s32[48]{0:T(128)S(1)} %multiply_add_fusion), kind=kOutput, calls=%fused_computation.14 | convolution fusion | flops 152572416 | bytes 4718784 | tf_op jit(solution)/shard_map/dot_general | solution.py:124
  15.1 3.6 %copy.38 = bf16[12,8,16,1024]{3,2,1,0:T(8,128)(2,1)} copy(bf16[12,8,16,1024]{3,1,2,0:T(8,128)(2,1)S(1)} %bitcast.75) | data formatting | bytes 6291456
  18.8 0.0 copy-start.3
  18.8 12.3 %all-to-all-start = ((bf16[32,3,16,1024]{3,2,1,0:T(8,128)(2,1)}), bf16[32,3,16,1024]{3,2,1,0:T(8,128)(2,1)}, u32[]{:S(2)}, u32[]{:S(2)}) async-start(bf16[32,3,16,1024]{3,2,1,0:T(8,128)(2,1)} %bitcast.74), calls=%async_computation | async-start | bytes 6291456 | tf_op jit(solution)/shard_map/all_to_all | solution.py:18
  31.0 0.0 all-gather.7.cloned.1.call-start
  31.1 0.0 copy-done.3
  31.1 2.9 %fusion.16 = f32[128,2048]{1,0:T(8,128)S(1)} fusion(bf16[128,1024]{1,0:T(8,128)(2,1)S(1)} %copy-done.3, bf16[1024,2048]{1,0:T(8,128)(2,1)} %param.12), kind=kOutput, calls=%fused_computation.40 | convolution fusion | flops 536870912 | bytes 5505024 | tf_op jit(solution)/shard_map/dot_general | solution.py:130
  34.0 0.0 copy-start.1
  34.0 1.0 copy-done.1
  35.0 0.1 multiply_convert_fusion.2
  35.2 12.3 %all-gather = bf16[256,1024]{1,0:T(8,128)(2,1)} all-gather(bf16[64,1024]{1,0:T(8,128)(2,1)S(1)} %get-tuple-element.69), channel_id=2, replica_groups=mesh['req'=32,'ctx_0'=4,'ctx_1'=2] {'ctx_0'}, dimensions={0}, use_global_device_ids=true | all-gather | bytes 655360 | tf_op jit(solution)/shard_map/all_gather | solution.py:39
  47.4 0.0 all-gather.7.cloned.1.call-update
  47.5 0.0 all-gather.9.cloned.1.call-start
  47.5 4.3 %all-gather.2 = bf16[128,1024]{1,0:T(8,128)(2,1)} all-gather(bf16[64,1024]{1,0:T(8,128)(2,1)S(1)} %get-tuple-element.70), channel_id=4, replica_groups=mesh['req'=32,'ctx_0'=4,'ctx_1'=2] {'ctx_1'}, dimensions={0}, use_global_device_ids=true | all-gather | bytes 393216 | tf_op jit(solution)/shard_map/all_gather | solution.py:39
  51.8 0.0 all-gather.9.cloned.1.call-update
  51.9 13.9 %all-gather.7.cloned.1.call-done = bf16[8,64,1024]{2,1,0:T(8,128)(2,1)} async-done(((bf16[4,64,1024]{2,1,0:T(8,128)(2,1)}), bf16[8,64,1024]{2,1,0:T(8,128)(2,1)}) %all-gather.7.cloned.1.call-update) | async-done | bytes 1048592 | tf_op jit(solution)/shard_map/all_gather | solution.py:39
  65.8 1.3 copy.25
  67.1 25.9 %all-gather.9.cloned.1.call-done = bf16[8,64,1024]{2,1,0:T(8,128)(2,1)} async-done(((bf16[2,64,1024]{2,1,0:T(8,128)(2,1)}), bf16[8,64,1024]{2,1,0:T(8,128)(2,1)}) %all-gather.9.cloned.1.call-update) | async-done | bytes 1048592 | tf_op jit(solution)/shard_map/all_gather | solution.py:39
  93.0 1.5 pad_maximum_fusion
  94.5 0.6 copy.40
  95.1 1.6 copy.27
  96.8 5.8 %all-to-all-done = bf16[32,3,16,1024]{3,2,1,0:T(8,128)(2,1)} async-done(((bf16[32,3,16,1024]{3,2,1,0:T(8,128)(2,1)}), bf16[32,3,16,1024]{3,2,1,0:T(8,128)(2,1)}, u32[]{:S(2)}, u32[]{:S(2)}) %all-to-all-start) | async-done | bytes 3145760 | tf_op jit(solution)/shard_map/all_to_all | solution.py:18
  102.6 9.5 %fusion.15 = f32[1536,2048]{1,0:T(8,128)S(1)} fusion(bf16[1536,1024]{1,0:T(8,128)(2,1)} %bitcast.1, bf16[1024,2048]{1,0:T(8,128)(2,1)} %param.11), kind=kOutput, calls=%fused_computation.39 | convolution fusion | flops 6442450944 | bytes 19922944 | tf_op jit(solution)/shard_map/dot_general | solution.py:117
  112.1 2.9 %multiply_convert_fusion = bf16[1536,1024]{1,0:T(8,128)(2,1)} fusion(f32[1536,2048]{1,0:T(8,128)S(1)} %fusion.15), kind=kLoop, calls=%fused_computation.17 | loop fusion | flops 7864320 | bytes 9437184 | tf_op jit(solution)/shard_map/convert
  115.1 0.5 slice.41
  115.6 3.9 %maximum_bitcast_fusion = bf16[192,8,16,128]{3,1,2,0:T(8,128)(2,1)S(1)} fusion(bf16[1536,1024]{1,0:T(8,128)(2,1)S(1)} %slice.41, bf16[1536,1024]{1,0:T(8,128)(2,1)} %multiply_convert_fusion), kind=kLoop, calls=%fused_computation.16 | loop fusion | flops 12582912 | bytes 12582912
  119.4 5.0 %copy.39 = bf16[192,8,16,128]{3,2,1,0:T(8,128)(2,1)} copy(bf16[192,8,16,128]{3,1,2,0:T(8,128)(2,1)S(1)} %maximum_bitcast_fusion) | data formatting | bytes 12582912
  124.4 43.5 %while.11 = (s32[]{:T(128)}, f32[1024,8,128]{0,2,1:T(8,128)}, bf16[3,512,2,8,128]{4,3,2,1,0:T(8,128)(2,1)}, bf16[1024,8,128]{2,0,1:T(8,128)(2,1)}, s32[]{:T(128)}, /*index=5*/s32[]{:T(128)}) while((s32[]{:T(128)}, f32[1024,8,128]{0,2,1:T(8,128)}, bf16[3,512,2,8,128]{4,3,2,1,0:T(8,128)(2,1)}, bf16[1024,8,128]{2,0,1:T(8,128)(2,1)}, ...), condition=%wide.region_3.4_spmd.clone, body=%wide.region_2.3_spmd.clone.sunk | while | flops 2174746624 | bytes 20971604 | solution.py:95
  124.4 2.0 constant_dynamic-slice_fusion.2
  126.4 1.9 copy.45
  128.3 10.2 %bitcast_add_fusion.2 = f32[1024,8,128]{0,2,1:T(8,128)} fusion(f32[1024,8,128]{0,2,1:T(8,128)} %get-tuple-element.103, pred[]{:T(512)S(6)} %compare.3, bf16[1024,8,128]{2,0,1:T(8,128)(2,1)} %get-tuple-element.111, bf16[512,2,8,128]{3,0,2,1:T(8,128)(2,1)} %bitcast.72), kind=kOutput, calls=%fused_computation.6.clone.1 | convolution fusion | flops 2174746624 | bytes 12582913 | tf_op jit(solution)/shard_map/while/body/eval_jaxpr/hqk,khd->qhd/dot_general | solution.py:91
  138.5 2.0 constant_dynamic-slice_fusion.2
  140.5 1.9 copy.45
  142.4 10.9 %bitcast_add_fusion.2 = f32[1024,8,128]{0,2,1:T(8,128)} fusion(f32[1024,8,128]{0,2,1:T(8,128)} %get-tuple-element.103, pred[]{:T(512)S(6)} %compare.3, bf16[1024,8,128]{2,0,1:T(8,128)(2,1)} %get-tuple-element.111, bf16[512,2,8,128]{3,0,2,1:T(8,128)(2,1)} %bitcast.72), kind=kOutput, calls=%fused_computation.6.clone.1 | convolution fusion | flops 2174746624 | bytes 12582913 | tf_op jit(solution)/shard_map/while/body/eval_jaxpr/hqk,khd->qhd/dot_general | solution.py:91
  153.2 2.0 constant_dynamic-slice_fusion.2
  155.2 1.9 copy.45
  157.1 10.9 %bitcast_add_fusion.2 = f32[1024,8,128]{0,2,1:T(8,128)} fusion(f32[1024,8,128]{0,2,1:T(8,128)} %get-tuple-element.103, pred[]{:T(512)S(6)} %compare.3, bf16[1024,8,128]{2,0,1:T(8,128)(2,1)} %get-tuple-element.111, bf16[512,2,8,128]{3,0,2,1:T(8,128)(2,1)} %bitcast.72), kind=kOutput, calls=%fused_computation.6.clone.1 | convolution fusion | flops 2174746624 | bytes 12582913 | tf_op jit(solution)/shard_map/while/body/eval_jaxpr/hqk,khd->qhd/dot_general | solution.py:91
  168.0 2.5 %convert_element_type.42 = bf16[1024,8,128]{0,2,1:T(8,128)(2,1)S(1)} convert(f32[1024,8,128]{0,2,1:T(8,128)} %get-tuple-element.27) | non-fusion elementwise | flops 1048576 | bytes 6291456 | tf_op jit(solution)/shard_map/convert_element_type | solution.py:134
  170.5 0.6 copy.41
  171.1 0.3 copy.29
  171.4 0.0 copy-start.2
  171.4 0.0 copy-start.4
  171.4 34.4 %all_to_all.10 = bf16[8,128,1024]{1,2,0:T(8,128)(2,1)S(1)} all-to-all(bf16[8,128,1024]{1,2,0:T(8,128)(2,1)S(1)} %copy.29), channel_id=1, replica_groups=mesh['req'=32,'ctx_0'=4,'ctx_1'=2] {'ctx_0','ctx_1'}, dimensions={0} | all-to-all | bytes 4194304 | tf_op jit(solution)/shard_map/all_to_all | solution.py:71
  205.8 2.4 %convert_reduce_fusion = (f32[128]{0:T(128)S(1)}, f32[128,1024]{0,1:T(8,128)}) fusion(bf16[8,128,1024]{1,2,0:T(8,128)(2,1)S(1)} %all_to_all.10), kind=kLoop, calls=%fused_computation.18 | loop fusion | flops 3014528 | bytes 2621952 | tf_op jit(solution)/shard_map/reduce_sum | solution.py:135
  208.2 2.0 copy.31
  210.2 1.2 multiply_reduce_fusion
  211.5 0.0 copy-done
  211.5 0.0 copy-done.2
  211.5 0.0 copy-done.4
  211.5 2.3 %fusion.7 = bf16[128,1024]{1,0:T(8,128)(2,1)} fusion(bf16[1024,1024]{1,0:T(8,128)(2,1)S(1)} %copy-done, bf16[128,1024]{1,0:T(8,128)(2,1)S(1)} %copy-done.4, f32[128,2048]{1,0:T(8,128)S(1)} %copy-done.2, f32[128,1024]{1,0:T(8,128)} %copy.31, f32[128]{0:T(128)S(1)} %add_rsqrt_fusion, f32[128]{0:T(128)S(1)} %broadcast_multiply_fusion), kind=kOutput, calls=%fused_computation.22 | convolution fusion | flops 269877248 | bytes 3671040 | tf_op jit(solution)/shard_map/dot_general | solution.py:139
  (4 shorter events, 0.0 us)
Async XLA Ops:
  6.5 205.0 %copy-start = (bf16[1024,1024]{1,0:T(8,128)(2,1)S(1)}, bf16[1024,1024]{1,0:T(8,128)(2,1)}, u32[]{:S(2)}) copy-start(bf16[1024,1024]{1,0:T(8,128)(2,1)} %param.13) | copy-start | bytes 6291460
  18.8 12.3 %copy-start.3 = (bf16[128,1024]{1,0:T(8,128)(2,1)S(1)}, bf16[128,1024]{1,0:T(8,128)(2,1)}, u32[]{:S(2)}) copy-start(bf16[128,1024]{1,0:T(8,128)(2,1)} %param.10) | copy-start | bytes 786436
  18.8 83.8 %all-to-all-start = ((bf16[32,3,16,1024]{3,2,1,0:T(8,128)(2,1)}), bf16[32,3,16,1024]{3,2,1,0:T(8,128)(2,1)}, u32[]{:S(2)}, u32[]{:S(2)}) async-start(bf16[32,3,16,1024]{3,2,1,0:T(8,128)(2,1)} %bitcast.74), calls=%async_computation | async-start | bytes 6291456 | tf_op jit(solution)/shard_map/all_to_all | solution.py:18
  31.0 34.7 %all-gather.7.cloned.1.call-start = ((), (), s32[]{:S(2)}) async-start(), calls=%async_computation.2 | async-start | bytes 1572864 | tf_op jit(solution)/shard_map/all_gather | solution.py:39
  34.0 1.0 copy-start.1
  47.5 45.5 %all-gather.9.cloned.1.call-start = ((), (), s32[]{:S(2)}) async-start(), calls=%async_computation.3 | async-start | bytes 1310720 | tf_op jit(solution)/shard_map/all_gather | solution.py:39
  171.4 40.1 %copy-start.2 = (f32[128,2048]{1,0:T(8,128)S(1)}, f32[128,2048]{1,0:T(8,128)}, u32[]{:S(2)}) copy-start(f32[128,2048]{1,0:T(8,128)} %copy-done.1) | copy-start | bytes 3145732
  171.4 40.1 %copy-start.4 = (bf16[128,1024]{1,0:T(8,128)(2,1)S(1)}, bf16[128,1024]{1,0:T(8,128)(2,1)}, u32[]{:S(2)}) copy-start(bf16[128,1024]{1,0:T(8,128)(2,1)} %param.10) | copy-start | bytes 786436
Sparse Core Ops, SparseCore 0:
  47.6 18.1 all-gather.6
  67.6 25.4 all-gather.8
where the time goes:
time: 221 us
  blocking collectives  51 us (23%)
  matrix products  49.1 us (22%)
  waiting for transfers between devices  45.7 us (21%)
  local copies, waits for them, and re-layouts  31.9 us (14%)
  other arithmetic  17 us (8%)
  between operations  13.6 us (6%)
  starting transfers between devices  12.4 us (6%)
    all_gather x2, waiting for transfers between devices, all_blocks(): parts = lax.all_gather(parts, axes[k])  39.8 us
    all_to_all x1, blocking collectives, sum_at_owner(): lax.all_to_all(cut_along(value, dim, length), axis, 0, 0, tiled=True)  34.4 us
    dot_general x3, matrix products, add_block(): jnp.einsum('hqk,khd->qhd', weights, piece[:, 1], preferred_element_type=j...  32 us
    all_gather x2, blocking collectives, all_blocks(): parts = lax.all_gather(parts, axes[k])  16.6 us
    unnamed x15, local copies, waits for them, and re-layouts  12.5 us
    all_to_all x1, starting transfers between devices, moved(): lax.all_to_all(group, axis, split_axis=split_dim, concat_axis=concat_dim,...  12.3 us
    dynamic_slice x6, local copies, waits for them, and re-layouts, attend(): lax.scan(add_block, jnp.zeros((count, heads, HEAD), jnp.float32), pieces)  11.5 us
    dot_general x1, matrix products, project(): linear = jnp.dot(flat, w_kv, preferred_element_type=jnp.float32)  9.54 us
  transfers between devices with their start and end apart: 3, of which 3 were waited for; matrix products, arithmetic and copies ran while one was open for 4% of the time, Pallas kernels for 0%

commit v1 on v0

v1 whole, which is shorter than its diff:
```python
import functools

import jax
import jax.numpy as jnp
from jax import lax
from jax.experimental import pallas as pl
from jax.experimental.pallas import tpu as pltpu
from jax.sharding import PartitionSpec as P

HEAD = 128
REQ_CTX = ("req", "ctx")
NY, NZ, NX = 4, 8, 4
CAP = 3
MESH = pl.DeviceIdType.MESH


def silu(v):
    half = 0.5 * v
    return half + half * jnp.tanh(half)


def chunk_dz(i):
    return 4 + lax.div(i + 1, 2) * (1 - 2 * lax.rem(i, 2))


def layer_kernel(
    owner_ref, hist_ref, cand_ref, wkv_ref, wqu_ref, wout_ref, out_ref,
    hist, cand, wkv, wqu, wout,
    send, recv, queries, gate, keys, values, acc,
    pair_out, pair_in, cross_out, cross_in, own,
    load_sem, send_sem, recv_sem, qsend_sem, qrecv_sem,
    psend_sem, precv_sem, xsend_sem, xrecv_sem,
):
    req, ctx = lax.axis_index("req"), lax.axis_index("ctx")
    y, z = lax.div(req, NZ), lax.rem(req, NZ)
    x, core = lax.div(ctx, 2), lax.rem(ctx, 2)
    rows, width = hist.shape
    blocks = owner_ref.shape[0]
    events = rows // blocks
    unit = CAP * events
    group = NY * unit
    cands = cand.shape[0]
    heads = width // HEAD

    loads = []
    for k, (src, dst) in enumerate(
        ((hist_ref, hist), (cand_ref, cand), (wqu_ref, wqu), (wkv_ref, wkv), (wout_ref, wout))
    ):
        copy = pltpu.make_async_copy(src, dst, load_sem.at[k])
        copy.start()
        loads.append(copy)

    barrier = pltpu.get_barrier_semaphore()
    for d in range(1, NY * NZ):
        pl.semaphore_signal(
            barrier, inc=1, device_id={"req": lax.rem(req + d, NY * NZ)}, device_id_type=MESH
        )
    for d in range(1, 2 * NX):
        pl.semaphore_signal(
            barrier, inc=1, device_id={"ctx": lax.rem(ctx + d, 2 * NX)}, device_id_type=MESH
        )

    owner = owner_ref[...].astype(jnp.float32)
    block_of = lax.div(lax.broadcasted_iota(jnp.int32, (blocks, rows), 1), events)
    earlier = lax.broadcasted_iota(jnp.int32, (blocks, rows), 0)
    owner_row = jnp.sum(jnp.where(earlier == block_of, owner, 0.0), axis=0, keepdims=True)
    same = jnp.logical_and(owner == owner_row, earlier < block_of)
    rank = jnp.sum(jnp.where(same, 1.0, 0.0), axis=0, keepdims=True)
    event = lax.rem(lax.broadcasted_iota(jnp.int32, (1, rows), 1), events)
    place = owner_row.astype(jnp.int32) * unit + rank.astype(jnp.int32) * events + event

    pl.semaphore_wait(barrier, NY * NZ + 2 * NX - 2)
    loads[0].wait()

    def exchange(i, j):
        to_y = lax.rem(y + j, NY)
        to_z = lax.rem(z + chunk_dz(i), NZ)
        spot = i * NY + j
        return pltpu.make_async_remote_copy(
            src_ref=send.at[pl.ds(pl.multiple_of(spot * unit, unit), unit)],
            dst_ref=recv.at[pl.ds(pl.multiple_of(spot * unit, unit), unit)],
            send_sem=send_sem.at[spot],
            recv_sem=recv_sem.at[spot],
            device_id={"req": to_y * NZ + to_z},
            device_id_type=MESH,
        )

    line = lax.broadcasted_iota(jnp.int32, (group, 1), 0)
    turn = sum(jnp.where(line >= unit * k, 1, 0) for k in range(1, NY))
    inside = line - turn * unit

    def pack(i):
        to_z = lax.rem(z + chunk_dz(i), NZ)
        target = (lax.rem(y + turn, NY) * NZ + to_z) * unit + inside
        placing = jnp.where(target == place, 1.0, 0.0).astype(jnp.bfloat16)
        return jnp.dot(placing, hist[...], preferred_element_type=jnp.float32).astype(jnp.bfloat16)

    last = NZ - 1

    @pl.loop(0, last)
    def _(i):
        send[pl.ds(pl.multiple_of(i * group, group), group), :] = pack(i)
        for j in range(NY):
            exchange(i, j).start()

    made = pack(last)
    recv[last * group : last * group + unit, :] = made[:unit]
    send[last * group + unit : (last + 1) * group, :] = made[unit:]
    for j in range(1, NY):
        exchange(last, j).start()

    loads[1].wait()
    loads[2].wait()
    mine = pl.ds(pl.multiple_of(ctx * cands, cands), cands)
    queries[mine, :] = silu(
        jnp.dot(cand[...], wqu[:, :width], preferred_element_type=jnp.float32)
    ).astype(jnp.bfloat16)

    def query_copy(d):
        return pltpu.make_async_remote_copy(
            src_ref=queries.at[mine],
            dst_ref=queries.at[mine],
            send_sem=qsend_sem.at[d],
            recv_sem=qrecv_sem.at[d],
            device_id={"ctx": lax.rem(ctx + d, 2 * NX)},
            device_id_type=MESH,
        )

    for d in range(1, 2 * NX):
        query_copy(d).start()
    gate[...] = silu(jnp.dot(cand[...], wqu[:, width:], preferred_element_type=jnp.float32))
    acc[...] = jnp.zeros_like(acc)
    loads[3].wait()

    def arrive(i):
        for j in range(NY):
            if j == 0:
                @pl.when(i < last)
                def _():
                    exchange(i, j).wait_recv()
            else:
                exchange(i, j).wait_recv()

    def project(i):
        events_in = recv[pl.ds(pl.multiple_of(i * group, group), group), :]
        keys[...] = silu(
            jnp.dot(events_in, wkv[:, :width], preferred_element_type=jnp.float32)
        ).astype(jnp.bfloat16)
        values[...] = jnp.dot(
            events_in, wkv[:, width:], preferred_element_type=jnp.float32
        ).astype(jnp.bfloat16)

    span = 2 * cands
    factor = 0.5 * HEAD ** (-0.5)

    def attend(at):
        here = pl.ds(pl.multiple_of(at * span, span), span)
        for h in range(heads):
            cols = slice(h * HEAD, (h + 1) * HEAD)
            scores = lax.dot_general(
                queries[here, cols], keys[:, cols], (((1,), (1,)), ((), ())),
                preferred_element_type=jnp.float32,
            )
            half = scores * factor
            weight = (half + half * jnp.tanh(half)).astype(jnp.bfloat16)
            acc[here, cols] += jnp.dot(
                weight, values[:, cols], preferred_element_type=jnp.float32
            )

    arrive(0)
    project(0)
    for d in range(1, 2 * NX):
        query_copy(d).wait_recv()

    @pl.loop(0, NX)
    def _(at):
        attend(at)

    @pl.loop(1, last)
    def _(i):
        arrive(i)
        project(i)

        @pl.loop(0, NX)
        def _(at):
            attend(at)

    arrive(last)
    project(last)

    def chip_at(i):
        return lax.rem(x + 2 + lax.div(i * (i + 1), 2), NX)

    def pair_copy(i):
        return pltpu.make_async_remote_copy(
            src_ref=pair_out.at[i],
            dst_ref=pair_in.at[i],
            send_sem=psend_sem.at[i],
            recv_sem=precv_sem.at[i],
            device_id={"ctx": 2 * x + 1 - core},
            device_id_type=MESH,
        )

    def cross_copy(i):
        return pltpu.make_async_remote_copy(
            src_ref=cross_out.at[i],
            dst_ref=cross_in.at[i],
            send_sem=xsend_sem.at[i],
            recv_sem=xrecv_sem.at[i],
            device_id={"ctx": 2 * chip_at(i) + core},
            device_id_type=MESH,
        )

    def part_of(i, which):
        at = 2 * chip_at(i) + which
        return acc[pl.ds(pl.multiple_of(at * cands, cands), cands), :]

    @pl.loop(0, NX)
    def _(i):
        attend(chip_at(i))
        pair_out[i] = part_of(i, 1 - core).astype(jnp.bfloat16)
        pair_copy(i).start()

    @pl.loop(0, NX - 1)
    def _(i):
        pair_copy(i).wait_recv()
        cross_out[i] = (part_of(i, core) + pair_in[i].astype(jnp.float32)).astype(jnp.bfloat16)
        cross_copy(i).start()

    pair_copy(NX - 1).wait_recv()
    own[...] = part_of(NX - 1, core) + pair_in[NX - 1].astype(jnp.float32)
    loads[4].wait()
    for i in (1, 2, 0):
        cross_copy(i).wait_recv()
    attended = own[...] + cross_in[0].astype(jnp.float32)
    attended = attended + cross_in[1].astype(jnp.float32) + cross_in[2].astype(jnp.float32)
    mean = jnp.mean(attended, axis=-1, keepdims=True)
    centred = attended - mean
    variance = jnp.mean(centred * centred, axis=-1, keepdims=True)
    mixed = (centred * lax.rsqrt(variance + 1e-05) * gate[...]).astype(jnp.bfloat16)
    result = cand[...].astype(jnp.float32) + jnp.dot(
        mixed, wout[...], preferred_element_type=jnp.float32
    )
    out_ref[...] = result.astype(jnp.bfloat16)

    @pl.loop(0, last)
    def _(i):
        for j in range(NY):
            exchange(i, j).wait_send()

    for j in range(1, NY):
        exchange(last, j).wait_send()
    for d in range(1, 2 * NX):
        query_copy(d).wait_send()
    for i in range(NX):
        pair_copy(i).wait_send()
    for i in range(NX - 1):
        cross_copy(i).wait_send()


def on_device(history, block_owner, candidates, w_kv, w_qu, w_out):
    rows, width = history.shape
    events = rows // block_owner.shape[0]
    cands = candidates.shape[0]
    group = NY * CAP * events
    total = NZ * group
    count = NY * NZ
    bf16, f32 = jnp.bfloat16, jnp.float32
    dma = pltpu.SemaphoreType.DMA
    anywhere = pl.BlockSpec(memory_space=pl.ANY)
    vmem = pl.BlockSpec(memory_space=pltpu.VMEM)
    return pl.pallas_call(
        layer_kernel,
        out_shape=jax.ShapeDtypeStruct((cands, width), bf16),
        in_specs=[vmem] + [anywhere] * 5,
        out_specs=vmem,
        scratch_shapes=[
            pltpu.VMEM((rows, width), bf16),
            pltpu.VMEM((cands, width), bf16),
            pltpu.VMEM((width, 2 * width), bf16),
            pltpu.VMEM((width, 2 * width), bf16),
            pltpu.VMEM((width, width), bf16),
            pltpu.VMEM((total, width), bf16),
            pltpu.VMEM((total, width), bf16),
            pltpu.VMEM((2 * NX * cands, width), bf16),
            pltpu.VMEM((cands, width), f32),
            pltpu.VMEM((group, width), bf16),
            pltpu.VMEM((group, width), bf16),
            pltpu.VMEM((2 * NX * cands, width), f32),
            pltpu.VMEM((NX, cands, width), bf16),
            pltpu.VMEM((NX, cands, width), bf16),
            pltpu.VMEM((NX - 1, cands, width), bf16),
            pltpu.VMEM((NX - 1, cands, width), bf16),
            pltpu.VMEM((cands, width), f32),
            dma((5,)),
            dma((count,)),
            dma((count,)),
            dma((2 * NX,)),
            dma((2 * NX,)),
            dma((NX,)),
            dma((NX,)),
            dma((NX - 1,)),
            dma((NX - 1,)),
        ],
        compiler_params=pltpu.CompilerParams(
            collective_id=0, has_side_effects=True, vmem_limit_bytes=60 * 2**20
        ),
    )(block_owner, history, candidates, w_kv, w_qu, w_out)


def solution(mesh):
    in_specs = (P(REQ_CTX, None), P(REQ_CTX, None), P(REQ_CTX, None), P(), P(), P())
    return jax.shard_map(
        on_device, mesh=mesh, in_specs=in_specs, out_specs=P(REQ_CTX, None), check_vma=False
    )
```

time: 221 us -> 119 us (0.54)
  Pallas kernels: 0 us -> 115 us
  blocking collectives: 51 us -> 0 us
  matrix products: 49.1 us -> 0 us
  waiting for transfers between devices: 45.7 us -> 0 us
  local copies, waits for them, and re-layouts: 31.9 us -> 3.02 us
  other arithmetic: 17 us -> 0 us
  between operations: 13.6 us -> 0.01 us
  starting transfers between devices: 12.4 us -> 0 us
    pallas_call x0 -> x1, Pallas kernels: none -> 115 us  [on_device(): pl.pallas_call(layer_kernel, out_shape=jax.ShapeDtypeStruct((cands, width...]
    dot_general x7 -> x0, matrix products: 49.1 us -> none  [the longest x3 32 us: add_block(): jnp.einsum('hqk,khd->qhd', weights, piece[:, 1], preferred_element_type=j...]
    all_gather x2 -> x0, waiting for transfers between devices: 39.8 us -> none  [all_blocks(): parts = lax.all_gather(parts, axes[k])]
    all_to_all x1 -> x0, blocking collectives: 34.4 us -> none  [sum_at_owner(): lax.all_to_all(cut_along(value, dim, length), axis, 0, 0, tiled=True)]
    all_gather x2 -> x0, blocking collectives: 16.6 us -> none  [all_blocks(): parts = lax.all_gather(parts, axes[k])]
    all_to_all x1 -> x0, starting transfers between devices: 12.3 us -> none  [moved(): lax.all_to_all(group, axis, split_axis=split_dim, concat_axis=concat_dim,...]
    dynamic_slice x6 -> x0, local copies, waits for them, and re-layouts: 11.5 us -> none  [attend(): lax.scan(add_block, jnp.zeros((count, heads, HEAD), jnp.float32), pieces)]
    unnamed x15 -> x2, local copies, waits for them, and re-layouts: 12.5 us -> 3.02 us
  transfers between devices with their start and end apart: 3 -> 0, of which waited for: 3 -> 0; matrix products, arithmetic and copies ran while one was open for 4% -> 0% of each run, Pallas kernels for 0% -> 0%
where the time goes in v1:
time: 119 us; the launch traced here: 118 us
  Pallas kernels  115 us (97%)
  local copies, waits for them, and re-layouts  3.02 us (3%)
    pallas_call x1, Pallas kernels, on_device(): pl.pallas_call(layer_kernel, out_shape=jax.ShapeDtypeStruct((cands, width...  115 us
    unnamed x2, local copies, waits for them, and re-layouts  3.02 us

profile of v1, /device:TPU:1, one launch (start us, length us, event | category | flops | bytes accessed | tf_op | source)
XLA Modules:
  0.0 118.3 jit_solution(9263346865343028564)
XLA Ops:
  0.0 1.3 %copy.7.owner_ref = s32[48,1]{1,0:T(8,128)} copy(s32[48,1]{0,1:T(1,128)} %param.7) | data formatting | bytes 384 | tf_op args[1]
  1.3 115.3 %shard_map.64 = bf16[128,1024]{1,0:T(8,128)(2,1)} custom-call(s32[48,1]{1,0:T(8,128)} %copy.7.owner_ref, bf16[768,1024]{1,0:T(8,128)(2,1)} %hist_ref.1, bf16[128,1024]{1,0:T(8,128)(2,1)} %cand_ref.1, bf16[1024,2048]{1,0:T(8,128)(2,1)} %wkv_ref.1, bf16[1024,2048]{1,0:T(8,128)(2,1)} %wqu_ref.1, bf16[1024,1024]{1,0:T(8,128)(2,1)} %wout_ref.1), custom_call_target="tpu_custom_call" | custom-call | tf_op jit(solution)/shard_map/pallas_call | solution.py:272
  116.6 1.7 %copy.9 = bf16[128,1024]{1,0:T(8,128)(2,1)} copy(bf16[128,1024]{1,0:T(8,128)(2,1)} %shard_map.64) | data formatting | bytes 524288

commit v2 on v1

--- a/solution.py
+++ b/solution.py
@@ -20,12 +20,12 @@
 
 
 def chunk_dz(i):
-    return 4 + lax.div(i + 1, 2) * (1 - 2 * lax.rem(i, 2))
+    return lax.rem(NZ + lax.div(i + 1, 2) * (2 * lax.rem(i, 2) - 1), NZ)
 
 
 def layer_kernel(
     owner_ref, hist_ref, cand_ref, wkv_ref, wqu_ref, wout_ref, out_ref,
-    hist, cand, wkv, wqu, wout,
+    owners, hist, cand, wkv, wqu, wout,
     send, recv, queries, gate, keys, values, acc,
     pair_out, pair_in, cross_out, cross_in, own,
     load_sem, send_sem, recv_sem, qsend_sem, qrecv_sem,
@@ -35,7 +35,7 @@
     y, z = lax.div(req, NZ), lax.rem(req, NZ)
     x, core = lax.div(ctx, 2), lax.rem(ctx, 2)
     rows, width = hist.shape
-    blocks = owner_ref.shape[0]
+    blocks = owner_ref.shape[1]
     events = rows // blocks
     unit = CAP * events
     group = NY * unit
@@ -44,7 +44,10 @@
 
     loads = []
     for k, (src, dst) in enumerate(
-        ((hist_ref, hist), (cand_ref, cand), (wqu_ref, wqu), (wkv_ref, wkv), (wout_ref, wout))
+        (
+            (owner_ref, owners), (hist_ref, hist), (cand_ref, cand),
+            (wqu_ref, wqu), (wkv_ref, wkv), (wout_ref, wout),
+        )
     ):
         copy = pltpu.make_async_copy(src, dst, load_sem.at[k])
         copy.start()
@@ -60,7 +63,11 @@
             barrier, inc=1, device_id={"ctx": lax.rem(ctx + d, 2 * NX)}, device_id_type=MESH
         )
 
-    owner = owner_ref[...].astype(jnp.float32)
+    loads[0].wait()
+    spot = lax.broadcasted_iota(jnp.int32, (blocks, blocks), 0)
+    diagonal = spot == lax.broadcasted_iota(jnp.int32, (blocks, blocks), 1)
+    listed = owners[...].astype(jnp.float32)
+    owner = jnp.sum(jnp.where(diagonal, listed, 0.0), axis=1, keepdims=True)
     block_of = lax.div(lax.broadcasted_iota(jnp.int32, (blocks, rows), 1), events)
     earlier = lax.broadcasted_iota(jnp.int32, (blocks, rows), 0)
     owner_row = jnp.sum(jnp.where(earlier == block_of, owner, 0.0), axis=0, keepdims=True)
@@ -69,8 +76,7 @@
     event = lax.rem(lax.broadcasted_iota(jnp.int32, (1, rows), 1), events)
     place = owner_row.astype(jnp.int32) * unit + rank.astype(jnp.int32) * events + event
 
-    pl.semaphore_wait(barrier, NY * NZ + 2 * NX - 2)
-    loads[0].wait()
+    loads[1].wait()
 
     def exchange(i, j):
         to_y = lax.rem(y + j, NY)
@@ -95,22 +101,24 @@
         placing = jnp.where(target == place, 1.0, 0.0).astype(jnp.bfloat16)
         return jnp.dot(placing, hist[...], preferred_element_type=jnp.float32).astype(jnp.bfloat16)
 
-    last = NZ - 1
-
-    @pl.loop(0, last)
+    last, early = NZ - 1, 3
+    made = pack(0)
+    recv[:unit, :] = made[:unit]
+    send[unit:group, :] = made[unit:]
+
+    @pl.loop(1, early)
     def _(i):
         send[pl.ds(pl.multiple_of(i * group, group), group), :] = pack(i)
+
+    pl.semaphore_wait(barrier, NY * NZ + 2 * NX - 2)
+    for i in range(1, early):
         for j in range(NY):
             exchange(i, j).start()
-
-    made = pack(last)
-    recv[last * group : last * group + unit, :] = made[:unit]
-    send[last * group + unit : (last + 1) * group, :] = made[unit:]
     for j in range(1, NY):
-        exchange(last, j).start()
-
-    loads[1].wait()
+        exchange(0, j).start()
+
     loads[2].wait()
+    loads[3].wait()
     mine = pl.ds(pl.multiple_of(ctx * cands, cands), cands)
     queries[mine, :] = silu(
         jnp.dot(cand[...], wqu[:, :width], preferred_element_type=jnp.float32)
@@ -128,18 +136,20 @@
 
     for d in range(1, 2 * NX):
         query_copy(d).start()
+
+    @pl.loop(early, NZ)
+    def _(i):
+        send[pl.ds(pl.multiple_of(i * group, group), group), :] = pack(i)
+        for j in range(NY):
+            exchange(i, j).start()
+
     gate[...] = silu(jnp.dot(cand[...], wqu[:, width:], preferred_element_type=jnp.float32))
     acc[...] = jnp.zeros_like(acc)
-    loads[3].wait()
+    loads[4].wait()
 
     def arrive(i):
         for j in range(NY):
-            if j == 0:
-                @pl.when(i < last)
-                def _():
-                    exchange(i, j).wait_recv()
-            else:
-                exchange(i, j).wait_recv()
+            exchange(i, j).wait_recv()
 
     def project(i):
         events_in = recv[pl.ds(pl.multiple_of(i * group, group), group), :]
@@ -167,7 +177,8 @@
                 weight, values[:, cols], preferred_element_type=jnp.float32
             )
 
-    arrive(0)
+    for j in range(1, NY):
+        exchange(0, j).wait_recv()
     project(0)
     for d in range(1, 2 * NX):
         query_copy(d).wait_recv()
@@ -215,21 +226,24 @@
         at = 2 * chip_at(i) + which
         return acc[pl.ds(pl.multiple_of(at * cands, cands), cands), :]
 
+    def cross(i):
+        pair_copy(i).wait_recv()
+        cross_out[i] = (part_of(i, core) + pair_in[i].astype(jnp.float32)).astype(jnp.bfloat16)
+        cross_copy(i).start()
+
     @pl.loop(0, NX)
     def _(i):
         attend(chip_at(i))
         pair_out[i] = part_of(i, 1 - core).astype(jnp.bfloat16)
         pair_copy(i).start()
 
-    @pl.loop(0, NX - 1)
-    def _(i):
-        pair_copy(i).wait_recv()
-        cross_out[i] = (part_of(i, core) + pair_in[i].astype(jnp.float32)).astype(jnp.bfloat16)
-        cross_copy(i).start()
+        @pl.when(i > 0)
+        def _():
+            cross(i - 1)
 
     pair_copy(NX - 1).wait_recv()
     own[...] = part_of(NX - 1, core) + pair_in[NX - 1].astype(jnp.float32)
-    loads[4].wait()
+    loads[5].wait()
     for i in (1, 2, 0):
         cross_copy(i).wait_recv()
     attended = own[...] + cross_in[0].astype(jnp.float32)
@@ -243,13 +257,14 @@
     )
     out_ref[...] = result.astype(jnp.bfloat16)
 
-    @pl.loop(0, last)
+    for j in range(1, NY):
+        exchange(0, j).wait_send()
+
+    @pl.loop(1, NZ)
     def _(i):
         for j in range(NY):
             exchange(i, j).wait_send()
 
-    for j in range(1, NY):
-        exchange(last, j).wait_send()
     for d in range(1, 2 * NX):
         query_copy(d).wait_send()
     for i in range(NX):
@@ -260,7 +275,8 @@
 
 def on_device(history, block_owner, candidates, w_kv, w_qu, w_out):
     rows, width = history.shape
-    events = rows // block_owner.shape[0]
+    blocks = block_owner.shape[0]
+    events = rows // blocks
     cands = candidates.shape[0]
     group = NY * CAP * events
     total = NZ * group
@@ -272,9 +288,10 @@
     return pl.pallas_call(
         layer_kernel,
         out_shape=jax.ShapeDtypeStruct((cands, width), bf16),
-        in_specs=[vmem] + [anywhere] * 5,
+        in_specs=[anywhere] * 6,
         out_specs=vmem,
         scratch_shapes=[
+            pltpu.VMEM((1, blocks), jnp.int32),
             pltpu.VMEM((rows, width), bf16),
             pltpu.VMEM((cands, width), bf16),
             pltpu.VMEM((width, 2 * width), bf16),
@@ -292,7 +309,7 @@
             pltpu.VMEM((NX - 1, cands, width), bf16),
             pltpu.VMEM((NX - 1, cands, width), bf16),
             pltpu.VMEM((cands, width), f32),
-            dma((5,)),
+            dma((6,)),
             dma((count,)),
             dma((count,)),
             dma((2 * NX,)),
@@ -305,7 +322,7 @@
         compiler_params=pltpu.CompilerParams(
             collective_id=0, has_side_effects=True, vmem_limit_bytes=60 * 2**20
         ),
-    )(block_owner, history, candidates, w_kv, w_qu, w_out)
+    )(block_owner.reshape(1, blocks), history, candidates, w_kv, w_qu, w_out)
 
 
 def solution(mesh):

time: 119 us -> 108 us (0.908)
  the two profiles are of different devices: /device:TPU:1 before, /device:TPU:19 now
where the time goes in v2:
time: 108 us
  Pallas kernels  106 us (98%)
  local copies, waits for them, and re-layouts  1.67 us (2%)
    pallas_call x1, Pallas kernels, on_device(): pl.pallas_call(layer_kernel, out_shape=jax.ShapeDtypeStruct((cands, width...  106 us

profile of v2, /device:TPU:19, one launch (start us, length us, event | category | flops | bytes accessed | tf_op | source)
XLA Modules:
  0.0 107.7 jit_solution(10551149288969551345)
XLA Ops:
  0.0 106.0 %shard_map.64 = bf16[128,1024]{1,0:T(8,128)(2,1)} custom-call(s32[1,48]{1,0:T(1,128)} %bitcast.1, bf16[768,1024]{1,0:T(8,128)(2,1)} %hist_ref.1, bf16[128,1024]{1,0:T(8,128)(2,1)} %cand_ref.1, bf16[1024,2048]{1,0:T(8,128)(2,1)} %wkv_ref.1, bf16[1024,2048]{1,0:T(8,128)(2,1)} %wqu_ref.1, bf16[1024,1024]{1,0:T(8,128)(2,1)} %wout_ref.1), custom_call_target="tpu_custom_call" | custom-call | tf_op jit(solution)/shard_map/pallas_call | solution.py:288
  106.0 1.7 %copy.8 = bf16[128,1024]{1,0:T(8,128)(2,1)} copy(bf16[128,1024]{1,0:T(8,128)(2,1)} %shard_map.64) | data formatting | bytes 524288

commit v3 on v2

--- a/solution.py
+++ b/solution.py
@@ -49,9 +49,9 @@
             (wqu_ref, wqu), (wkv_ref, wkv), (wout_ref, wout),
         )
     ):
-        copy = pltpu.make_async_copy(src, dst, load_sem.at[k])
-        copy.start()
-        loads.append(copy)
+        loads.append(pltpu.make_async_copy(src, dst, load_sem.at[k]))
+    loads[0].start()
+    loads[1].start()
 
     barrier = pltpu.get_barrier_semaphore()
     for d in range(1, NY * NZ):
@@ -77,6 +77,8 @@
     place = owner_row.astype(jnp.int32) * unit + rank.astype(jnp.int32) * events + event
 
     loads[1].wait()
+    for copy in loads[2:]:
+        copy.start()
 
     def exchange(i, j):
         to_y = lax.rem(y + j, NY)
@@ -102,18 +104,22 @@
         return jnp.dot(placing, hist[...], preferred_element_type=jnp.float32).astype(jnp.bfloat16)
 
     last, early = NZ - 1, 3
+    turns = (1, 3, 0, 2)
+
+    def fill(i):
+        send[pl.ds(pl.multiple_of(i * group, group), group), :] = pack(i)
+
+    @pl.loop(1, early)
+    def _(i):
+        fill(i)
+
+    pl.semaphore_wait(barrier, NY * NZ + 2 * NX - 2)
+    for j in turns:
+        for i in range(1, early):
+            exchange(i, j).start()
     made = pack(0)
     recv[:unit, :] = made[:unit]
     send[unit:group, :] = made[unit:]
-
-    @pl.loop(1, early)
-    def _(i):
-        send[pl.ds(pl.multiple_of(i * group, group), group), :] = pack(i)
-
-    pl.semaphore_wait(barrier, NY * NZ + 2 * NX - 2)
-    for i in range(1, early):
-        for j in range(NY):
-            exchange(i, j).start()
     for j in range(1, NY):
         exchange(0, j).start()
 
@@ -137,11 +143,21 @@
     for d in range(1, 2 * NX):
         query_copy(d).start()
 
-    @pl.loop(early, NZ)
-    def _(i):
-        send[pl.ds(pl.multiple_of(i * group, group), group), :] = pack(i)
-        for j in range(NY):
-            exchange(i, j).start()
+    @pl.loop(0, (last - early) // 2)
+    def _(p):
+        first = early + 2 * p
+
+        @pl.loop(first, first + 2)
+        def _(i):
+            fill(i)
+
+        for j in turns:
+            exchange(first, j).start()
+            exchange(first + 1, j).start()
+
+    fill(last)
+    for j in turns:
+        exchange(last, j).start()
 
     gate[...] = silu(jnp.dot(cand[...], wqu[:, width:], preferred_element_type=jnp.float32))
     acc[...] = jnp.zeros_like(acc)
@@ -212,24 +228,46 @@
             device_id_type=MESH,
         )
 
-    def cross_copy(i):
+    half_width = width // 2
+
+    def cross_copy(kind, way):
         return pltpu.make_async_remote_copy(
-            src_ref=cross_out.at[i],
-            dst_ref=cross_in.at[i],
-            send_sem=xsend_sem.at[i],
-            recv_sem=xrecv_sem.at[i],
-            device_id={"ctx": 2 * chip_at(i) + core},
+            src_ref=cross_out.at[kind, way],
+            dst_ref=cross_in.at[kind, way],
+            send_sem=xsend_sem.at[kind, way],
+            recv_sem=xrecv_sem.at[kind, way],
+            device_id={"ctx": 2 * lax.rem(x + (1 if way == 0 else NX - 1), NX) + core},
             device_id_type=MESH,
         )
+
+    def columns(k):
+        return slice(k * half_width, (k + 1) * half_width)
 
     def part_of(i, which):
         at = 2 * chip_at(i) + which
         return acc[pl.ds(pl.multiple_of(at * cands, cands), cands), :]
 
-    def cross(i):
+    def summed(i):
         pair_copy(i).wait_recv()
-        cross_out[i] = (part_of(i, core) + pair_in[i].astype(jnp.float32)).astype(jnp.bfloat16)
-        cross_copy(i).start()
+        return part_of(i, core) + pair_in[i].astype(jnp.float32)
+
+    def hand_on():
+        both = summed(0).astype(jnp.bfloat16)
+        for way in (0, 1):
+            cross_out[0, way] = both[:, columns(way)]
+            cross_copy(0, way).start()
+
+    def direct(i, way):
+        own[way] = summed(i)
+        cross_out[2, way] = own[way][:, columns(1 - way)].astype(jnp.bfloat16)
+        cross_copy(2, way).start()
+
+    def relay(way):
+        cross_copy(0, way).wait_recv()
+        cross_out[1, way] = (
+            own[way][:, columns(way)] + cross_in[0, way].astype(jnp.float32)
+        ).astype(jnp.bfloat16)
+        cross_copy(1, way).start()
 
     @pl.loop(0, NX)
     def _(i):
@@ -237,17 +275,30 @@
         pair_out[i] = part_of(i, 1 - core).astype(jnp.bfloat16)
         pair_copy(i).start()
 
-        @pl.when(i > 0)
+        @pl.when(i == 1)
         def _():
-            cross(i - 1)
-
-    pair_copy(NX - 1).wait_recv()
-    own[...] = part_of(NX - 1, core) + pair_in[NX - 1].astype(jnp.float32)
+            hand_on()
+
+        @pl.when(i == 2)
+        def _():
+            direct(1, 1)
+
+        @pl.when(i == 3)
+        def _():
+            direct(2, 0)
+
+    relay(1)
+    relay(0)
+    total = summed(NX - 1)
     loads[5].wait()
-    for i in (1, 2, 0):
-        cross_copy(i).wait_recv()
-    attended = own[...] + cross_in[0].astype(jnp.float32)
-    attended = attended + cross_in[1].astype(jnp.float32) + cross_in[2].astype(jnp.float32)
+    for kind in (2, 1):
+        for way in (0, 1):
+            cross_copy(kind, way).wait_recv()
+    sides = [
+        cross_in[1, way].astype(jnp.float32) + cross_in[2, 1 - way].astype(jnp.float32)
+        for way in (0, 1)
+    ]
+    attended = total + jnp.concatenate(sides, axis=1)
     mean = jnp.mean(attended, axis=-1, keepdims=True)
     centred = attended - mean
     variance = jnp.mean(centred * centred, axis=-1, keepdims=True)
@@ -269,8 +320,9 @@
         query_copy(d).wait_send()
     for i in range(NX):
         pair_copy(i).wait_send()
-    for i in range(NX - 1):
-        cross_copy(i).wait_send()
+    for kind in range(3):
+        for way in (0, 1):
+            cross_copy(kind, way).wait_send()
 
 
 def on_device(history, block_owner, candidates, w_kv, w_qu, w_out):
@@ -306,9 +358,9 @@
             pltpu.VMEM((2 * NX * cands, width), f32),
             pltpu.VMEM((NX, cands, width), bf16),
             pltpu.VMEM((NX, cands, width), bf16),
-            pltpu.VMEM((NX - 1, cands, width), bf16),
-            pltpu.VMEM((NX - 1, cands, width), bf16),
-            pltpu.VMEM((cands, width), f32),
+            pltpu.VMEM((3, 2, cands, width // 2), bf16),
+            pltpu.VMEM((3, 2, cands, width // 2), bf16),
+            pltpu.VMEM((2, cands, width), f32),
             dma((6,)),
             dma((count,)),
             dma((count,)),
@@ -316,8 +368,8 @@
             dma((2 * NX,)),
             dma((NX,)),
             dma((NX,)),
-            dma((NX - 1,)),
-            dma((NX - 1,)),
+            dma((3, 2)),
+            dma((3, 2)),
         ],
         compiler_params=pltpu.CompilerParams(
             collective_id=0, has_side_effects=True, vmem_limit_bytes=60 * 2**20

time: 108 us -> 112 us (1.037)
  the two profiles are of different devices: /device:TPU:19 before, /device:TPU:1 now
where the time goes in v3:
time: 112 us
  Pallas kernels  110 us (98%)
  local copies, waits for them, and re-layouts  1.67 us (1%)
    pallas_call x1, Pallas kernels, on_device(): pl.pallas_call(layer_kernel, out_shape=jax.ShapeDtypeStruct((cands, width...  110 us

profile of v3, /device:TPU:1, one launch (start us, length us, event | category | flops | bytes accessed | tf_op | source)
XLA Modules:
  0.0 111.6 jit_solution(3043107499592942345)
XLA Ops:
  0.0 109.9 %shard_map.64 = bf16[128,1024]{1,0:T(8,128)(2,1)} custom-call(s32[1,48]{1,0:T(1,128)} %bitcast.1, bf16[768,1024]{1,0:T(8,128)(2,1)} %hist_ref.1, bf16[128,1024]{1,0:T(8,128)(2,1)} %cand_ref.1, bf16[1024,2048]{1,0:T(8,128)(2,1)} %wkv_ref.1, bf16[1024,2048]{1,0:T(8,128)(2,1)} %wqu_ref.1, bf16[1024,1024]{1,0:T(8,128)(2,1)} %wout_ref.1), custom_call_target="tpu_custom_call" | custom-call | tf_op jit(solution)/shard_map/pallas_call | solution.py:340
  109.9 1.7 %copy.8 = bf16[128,1024]{1,0:T(8,128)(2,1)} copy(bf16[128,1024]{1,0:T(8,128)(2,1)} %shard_map.64) | data formatting | bytes 524288

commit v4 on v3

--- a/solution.py
+++ b/solution.py
@@ -49,9 +49,9 @@
             (wqu_ref, wqu), (wkv_ref, wkv), (wout_ref, wout),
         )
     ):
-        loads.append(pltpu.make_async_copy(src, dst, load_sem.at[k]))
-    loads[0].start()
-    loads[1].start()
+        copy = pltpu.make_async_copy(src, dst, load_sem.at[k])
+        copy.start()
+        loads.append(copy)
 
     barrier = pltpu.get_barrier_semaphore()
     for d in range(1, NY * NZ):
@@ -77,8 +77,6 @@
     place = owner_row.astype(jnp.int32) * unit + rank.astype(jnp.int32) * events + event
 
     loads[1].wait()
-    for copy in loads[2:]:
-        copy.start()
 
     def exchange(i, j):
         to_y = lax.rem(y + j, NY)
@@ -104,22 +102,18 @@
         return jnp.dot(placing, hist[...], preferred_element_type=jnp.float32).astype(jnp.bfloat16)
 
     last, early = NZ - 1, 3
-    turns = (1, 3, 0, 2)
-
-    def fill(i):
-        send[pl.ds(pl.multiple_of(i * group, group), group), :] = pack(i)
-
-    @pl.loop(1, early)
-    def _(i):
-        fill(i)
-
-    pl.semaphore_wait(barrier, NY * NZ + 2 * NX - 2)
-    for j in turns:
-        for i in range(1, early):
-            exchange(i, j).start()
     made = pack(0)
     recv[:unit, :] = made[:unit]
     send[unit:group, :] = made[unit:]
+
+    @pl.loop(1, early)
+    def _(i):
+        send[pl.ds(pl.multiple_of(i * group, group), group), :] = pack(i)
+
+    pl.semaphore_wait(barrier, NY * NZ + 2 * NX - 2)
+    for i in range(1, early):
+        for j in range(NY):
+            exchange(i, j).start()
     for j in range(1, NY):
         exchange(0, j).start()
 
@@ -143,21 +137,11 @@
     for d in range(1, 2 * NX):
         query_copy(d).start()
 
-    @pl.loop(0, (last - early) // 2)
-    def _(p):
-        first = early + 2 * p
-
-        @pl.loop(first, first + 2)
-        def _(i):
-            fill(i)
-
-        for j in turns:
-            exchange(first, j).start()
-            exchange(first + 1, j).start()
-
-    fill(last)
-    for j in turns:
-        exchange(last, j).start()
+    @pl.loop(early, NZ)
+    def _(i):
+        send[pl.ds(pl.multiple_of(i * group, group), group), :] = pack(i)
+        for j in range(NY):
+            exchange(i, j).start()
 
     gate[...] = silu(jnp.dot(cand[...], wqu[:, width:], preferred_element_type=jnp.float32))
     acc[...] = jnp.zeros_like(acc)

time: 112 us -> 106 us (0.946)
  the two profiles are of different devices: /device:TPU:1 before, /device:TPU:16 now
where the time goes in v4:
time: 106 us
  Pallas kernels  104 us (98%)
  local copies, waits for them, and re-layouts  1.67 us (2%)
    pallas_call x1, Pallas kernels, on_device(): pl.pallas_call(layer_kernel, out_shape=jax.ShapeDtypeStruct((cands, width...  104 us

profile of v4, /device:TPU:16, one launch (start us, length us, event | category | flops | bytes accessed | tf_op | source)
XLA Modules:
  0.0 105.5 jit_solution(10008486656421948601)
XLA Ops:
  0.0 103.8 %shard_map.64 = bf16[128,1024]{1,0:T(8,128)(2,1)} custom-call(s32[1,48]{1,0:T(1,128)} %bitcast.1, bf16[768,1024]{1,0:T(8,128)(2,1)} %hist_ref.1, bf16[128,1024]{1,0:T(8,128)(2,1)} %cand_ref.1, bf16[1024,2048]{1,0:T(8,128)(2,1)} %wkv_ref.1, bf16[1024,2048]{1,0:T(8,128)(2,1)} %wqu_ref.1, bf16[1024,1024]{1,0:T(8,128)(2,1)} %wout_ref.1), custom_call_target="tpu_custom_call" | custom-call | tf_op jit(solution)/shard_map/pallas_call | solution.py:324
  103.8 1.7 %copy.8 = bf16[128,1024]{1,0:T(8,128)(2,1)} copy(bf16[128,1024]{1,0:T(8,128)(2,1)} %shard_map.64) | data formatting | bytes 524288
